TPU v7x, 32 devices: a whole 2x2x4 slice. The times are simulated.
32 devices in a mesh: lat: 4 (over y, x), lon: 4 (over z), mem: 2 (over core).
Axes of the slice: x: 2, y: 2, z: 4, core: 2. Of those that a mesh axis runs over, the one named last changes fastest.
Arguments:
- anomalies: bfloat16 [24, 4, 1440, 512], P('mem', None, 'lon', 'lat'), may hold values from -6 to 6
- taper: float32 [4, 1440, 512], P('lon', 'lat'), may hold values from 0.5 to 8
- obs_row: int32 [256, 512], P('lat', 'lon'), may hold values from 0 to 511, as said below
- obs_col: int32 [256, 512], P('lat', 'lon'), may hold values from 0 to 1439, as said below
- obs_level: int32 [256, 512], P('lat', 'lon'), may hold values from 0 to 3
- obs_value: float32 [256, 512], P('lat', 'lon'), may hold values from -18 to 18
Outputs:
- increment: float32 [4, 1440, 512], P(None, 'lon', 'lat')
Inputs may be any that keep to these rules, and one draw needn't show every extreme that they name: `obs_row`: the entry in row i lies in latitude rows (i // 64) * 128 to (i // 64 + 1) * 128 - 1, drawn evenly there. `obs_col`: the entry in column j lies in longitude columns (j // 128) * 360 to (j // 128 + 1) * 360 - 1, drawn evenly there.
All inputs are finite; a program needn't handle non-finite values.
Results may differ from a plain program's by a relative error of at most 0.0066.
Values may be sent and summed in bfloat16 or wider, within the bound.
A program may use at most 128 MiB of HBM per device.

v0:
```python
import math

import jax
import jax.numpy as jnp
from jax import lax
from jax.sharding import PartitionSpec as P


def lon_basis(length):
    grid_idx = jnp.arange(length, dtype=jnp.int32)[:, None]
    coef_idx = jnp.arange(length, dtype=jnp.int32)[None, :]
    nyquist = length // 2
    wavenum = jnp.where(coef_idx <= nyquist, coef_idx, coef_idx - nyquist)
    phase_idx = grid_idx * wavenum % length
    angles = phase_idx.astype(jnp.float32) * (2.0 * math.pi / length)
    scales = jnp.where(
        (coef_idx == 0) | (coef_idx == nyquist), 1.0 / math.sqrt(length), math.sqrt(2.0 / length)
    )
    basis = jnp.where(coef_idx <= nyquist, jnp.cos(angles), jnp.sin(angles)) * scales
    return basis.astype(jnp.bfloat16)


def lat_basis(length):
    grid_idx = jnp.arange(length, dtype=jnp.int32)[:, None]
    mode_idx = jnp.arange(length, dtype=jnp.int32)[None, :]
    phase_idx = mode_idx * (2 * grid_idx + 1) % (4 * length)
    angles = phase_idx.astype(jnp.float32) * (math.pi / (2.0 * length))
    scales = jnp.where(mode_idx == 0, 1.0 / math.sqrt(length), math.sqrt(2.0 / length))
    return (jnp.cos(angles) * scales).astype(jnp.bfloat16)


def spread_observations(cell_keys, row_local, obs_value, slot_count, row_count):
    obs_count = cell_keys.size
    block_rows = min(obs_count, 2048)
    turn_count = obs_count // block_rows
    key_blocks = cell_keys.reshape(turn_count, block_rows)
    row_blocks = row_local.reshape(turn_count, block_rows)
    value_blocks = obs_value.reshape(turn_count, block_rows)
    slot_ids = jnp.arange(slot_count, dtype=jnp.int32)
    row_ids = jnp.arange(row_count, dtype=jnp.int32)

    def add_block(running, obs_block):
        key_part, row_part, value_part = obs_block
        left_hot = (key_part[:, None] == slot_ids[None, :]).astype(jnp.bfloat16)
        high_part = value_part.astype(jnp.bfloat16)
        remainder = value_part - high_part.astype(jnp.float32)
        middle_part = remainder.astype(jnp.bfloat16)
        low_part = (remainder - middle_part.astype(jnp.float32)).astype(jnp.bfloat16)
        pieces = jnp.stack([high_part, middle_part, low_part], axis=1)
        row_hits = (row_part[:, None] == row_ids[None, :]).astype(jnp.bfloat16)
        weighted_rows = (pieces[:, :, None] * row_hits[:, None, :]).reshape(
            block_rows, 3 * row_count
        )
        added = jnp.einsum("ok,oz->kz", left_hot, weighted_rows, preferred_element_type=jnp.float32)
        return (running + added, None)

    start_sum = jnp.zeros((slot_count, 3 * row_count), jnp.float32)
    running, _ = lax.scan(add_block, start_sum, (key_blocks, row_blocks, value_blocks))
    return jnp.sum(running.reshape(slot_count, 3, row_count), axis=1)


def local(anomalies, taper, obs_row, obs_col, obs_level, obs_value):
    member_count, level_count, col_count, row_count = anomalies.shape
    lon_total = col_count * lax.axis_size("lon")
    lat_total = row_count * lax.axis_size("lat")
    row_start = lax.axis_index("lat") * row_count
    col_start = lax.axis_index("lon") * col_count
    cell_keys = (obs_level * col_count + (obs_col - col_start)).reshape(-1)
    row_local = (obs_row - row_start).reshape(-1)
    innovation = spread_observations(
        cell_keys, row_local, obs_value.reshape(-1), level_count * col_count, row_count
    )
    innovation = innovation.reshape(level_count, col_count, row_count).astype(jnp.bfloat16)
    lon_table = lon_basis(lon_total)
    lat_table = lat_basis(lat_total)
    ensemble = member_count * lax.axis_size("mem")
    fields, innov_cols = (
        lax.all_to_all(anomalies, "lon", split_axis=1, concat_axis=2, tiled=True),
        lax.all_to_all(innovation[None], "lon", split_axis=1, concat_axis=2, tiled=True),
    )
    zonal_coef = jnp.einsum(
        "alxy,xk->alky", fields * innov_cols, lon_table, preferred_element_type=jnp.float32
    ).astype(jnp.bfloat16)
    modal_zonal_coef = lax.all_to_all(zonal_coef, "lat", split_axis=2, concat_axis=3, tiled=True)
    spectrum = jnp.einsum(
        "alky,yn->alkn", modal_zonal_coef, lat_table, preferred_element_type=jnp.float32
    )
    tapered = (spectrum * taper[None]).astype(jnp.bfloat16)
    filtered = jnp.einsum(
        "alkn,yn->alky", tapered, lat_table, preferred_element_type=jnp.float32
    ).astype(jnp.bfloat16)
    inverse = lax.all_to_all(filtered, "lat", split_axis=3, concat_axis=2, tiled=True)
    localized = jnp.einsum("alky,xk->alxy", inverse, lon_table, preferred_element_type=jnp.float32)
    local_sum = jnp.sum(fields.astype(jnp.float32) * localized, axis=0)
    merged = lax.psum(local_sum, "mem")
    summed = lax.all_to_all(merged, "lon", split_axis=1, concat_axis=0, tiled=True)
    return summed / (ensemble - 1)


def solution(mesh):
    in_specs = (
        P("mem", None, "lon", "lat"),
        P("lon", "lat", None),
        P("lat", "lon"),
        P("lat", "lon"),
        P("lat", "lon"),
        P("lat", "lon"),
    )
    out_specs = P(None, "lon", "lat")
    return jax.shard_map(local, mesh=mesh, in_specs=in_specs, out_specs=out_specs, check_vma=False)
```

profile of v0, /device:TPU:0, one launch (start us, length us, event | category | flops | bytes accessed | tf_op | source)
XLA Modules:
  0.0 481.3 jit_solution(4805282629353373172)
XLA Ops:
  6.5 4.6 copy.33
  11.1 6.5 %all-to-all-start = ((bf16[12,4,360,128]{3,2,0,1:T(8,128)(2,1)}), bf16[12,4,360,128]{3,2,0,1:T(8,128)(2,1)}, u32[]{:S(2)}, u32[]{:S(2)}) async-start(bf16[12,4,360,128]{3,2,0,1:T(8,128)(2,1)} %copy.33), calls=%async_computation | async-start | bytes 8847360 | tf_op jit(solution)/shard_map/all_to_all | solution.py:78
  17.7 27.3 %while.11 = (s32[]{:T(128)}, f32[1440,384]{1,0:T(8,128)}, s32[4,2048]{1,0:T(4,128)S(1)}, f32[4,2048]{1,0:T(4,128)S(1)}, s32[4,2048]{1,0:T(4,128)S(1)}, /*index=5*/s32[]{:T(128)}, s32[]{:T(128)}) while((s32[]{:T(128)}, f32[1440,384]{1,0:T(8,128)}, s32[4,2048]{1,0:T(4,128)S(1)}, f32[4,2048]{1,0:T(4,128)S(1)}, ...), condition=%wide.region_1.2_spmd.clone, body=%wide.region_0.1_spmd.clone.sunk | while | flops 2273290240 | bytes 8728675 | solution.py:58
  18.1 5.2 %fusion.95 = f32[1440,384]{1,0:T(8,128)} fusion(bf16[2048,384]{0,1:T(8,128)(2,1)S(1)} %bitcast.84, s32[2048]{0:T(1024)S(1)} %bitcast.91, f32[1440,384]{1,0:T(8,128)} %get-tuple-element.126, pred[]{:T(512)S(6)} %compare.4), kind=kOutput, calls=%fused_computation.6.clone.1 | convolution fusion | flops 2271928320 | bytes 6004737 | tf_op jit(solution)/shard_map/while/body/eval_jaxpr/ok,oz->kz/dot_general | solution.py:54
  23.7 6.8 %fusion.95 = f32[1440,384]{1,0:T(8,128)} fusion(bf16[2048,384]{0,1:T(8,128)(2,1)S(1)} %bitcast.84, s32[2048]{0:T(1024)S(1)} %bitcast.91, f32[1440,384]{1,0:T(8,128)} %get-tuple-element.126, pred[]{:T(512)S(6)} %compare.4), kind=kOutput, calls=%fused_computation.6.clone.1 | convolution fusion | flops 2271928320 | bytes 6004737 | tf_op jit(solution)/shard_map/while/body/eval_jaxpr/ok,oz->kz/dot_general | solution.py:54
  30.9 6.9 %fusion.95 = f32[1440,384]{1,0:T(8,128)} fusion(bf16[2048,384]{0,1:T(8,128)(2,1)S(1)} %bitcast.84, s32[2048]{0:T(1024)S(1)} %bitcast.91, f32[1440,384]{1,0:T(8,128)} %get-tuple-element.126, pred[]{:T(512)S(6)} %compare.4), kind=kOutput, calls=%fused_computation.6.clone.1 | convolution fusion | flops 2271928320 | bytes 6004737 | tf_op jit(solution)/shard_map/while/body/eval_jaxpr/ok,oz->kz/dot_general | solution.py:54
  38.2 6.8 %fusion.95 = f32[1440,384]{1,0:T(8,128)} fusion(bf16[2048,384]{0,1:T(8,128)(2,1)S(1)} %bitcast.84, s32[2048]{0:T(1024)S(1)} %bitcast.91, f32[1440,384]{1,0:T(8,128)} %get-tuple-element.126, pred[]{:T(512)S(6)} %compare.4), kind=kOutput, calls=%fused_computation.6.clone.1 | convolution fusion | flops 2271928320 | bytes 6004737 | tf_op jit(solution)/shard_map/while/body/eval_jaxpr/ok,oz->kz/dot_general | solution.py:54
  45.0 2.0 copy.36
  47.0 0.2 reduce_sum.20
  47.3 0.9 copy.37
  48.2 67.8 %all-to-all-done = bf16[12,4,360,128]{3,2,0,1:T(8,128)(2,1)} async-done(((bf16[12,4,360,128]{3,2,0,1:T(8,128)(2,1)}), bf16[12,4,360,128]{3,2,0,1:T(8,128)(2,1)}, u32[]{:S(2)}, u32[]{:S(2)}) %all-to-all-start) | async-done | bytes 4423712 | tf_op jit(solution)/shard_map/all_to_all | solution.py:78
  116.0 3.9 all-to-all-start.1
  119.9 39.0 %fusion.84 = bf16[1440,1440,1]{1,0,2:T(8,128)(2,1)} fusion(f32[1440]{0:T(1024)S(1)} %fusion.58, s32[1440]{0:T(1024)S(1)} %add_select_fusion.2, pred[1440]{0:T(1024)(128)(4,1)S(1)} %iota_compare_fusion.4), kind=kLoop, calls=%fused_computation.29.clone.clone.clone.clone.1 | loop fusion | flops 24883200 | bytes 4160160 | tf_op jit(solution)/shard_map/alxy,xk->alky/dot_general | solution.py:81
  158.9 4.7 copy.35
  163.6 2.9 bitcast_multiply_fusion.1
  166.5 0.7 copy-done.5
  167.2 7.6 %fusion.28 = bf16[12,1,1440,128]{3,2,0,1:T(8,128)(2,1)S(1)} fusion(bf16[12,1440,128]{2,1,0:T(8,128)(2,1)S(1)} %bitcast_multiply_fusion.1, bf16[1440,1440,1]{1,0,2:T(8,128)(2,1)S(1)} %copy-done.5), kind=kOutput, calls=%fused_computation.39 | convolution fusion | flops 6372311040 | bytes 12994560 | tf_op jit(solution)/shard_map/alxy,xk->alky/dot_general | solution.py:81
  174.8 12.3 %copy.40 = bf16[12,1,1440,128]{3,0,1,2:T(8,128)(2,1)} copy(bf16[12,1,1440,128]{3,2,0,1:T(8,128)(2,1)S(1)} %fusion.28) | data formatting | bytes 8847360 | tf_op jit(solution)/shard_map/convert_element_type | solution.py:83
  187.1 5.2 %all-to-all-start.2 = ((bf16[12,1,1440,128]{3,0,1,2:T(8,128)(2,1)}), bf16[12,1,1440,128]{3,0,1,2:T(8,128)(2,1)}, u32[]{:S(2)}, u32[]{:S(2)}) async-start(bf16[12,1,1440,128]{3,0,1,2:T(8,128)(2,1)} %copy.40), calls=%async_computation.2 | async-start | bytes 11796480 | tf_op jit(solution)/shard_map/all_to_all | solution.py:84
  192.3 65.0 %all-to-all-done.2 = bf16[12,1,1440,128]{3,0,1,2:T(8,128)(2,1)} async-done(((bf16[12,1,1440,128]{3,0,1,2:T(8,128)(2,1)}), bf16[12,1,1440,128]{3,0,1,2:T(8,128)(2,1)}, u32[]{:S(2)}, u32[]{:S(2)}) %all-to-all-start.2) | async-done | bytes 4423712 | tf_op jit(solution)/shard_map/all_to_all | solution.py:84
  257.3 8.2 %copy.47 = bf16[12,1,4,360,128]{4,2,3,0,1:T(4,128)(2,1)} copy(bf16[12,1,4,360,128]{4,0,3,2,1:T(8,128)(2,1)} %bitcast.10) | data formatting | bytes 8847360 | tf_op jit(solution)/shard_map/all_to_all | solution.py:84
  265.5 8.6 %reshape.193 = bf16[12,360,512]{2,1,0:T(8,128)(2,1)} reshape(bf16[12,1,360,4,128]{4,3,2,0,1:T(4,128)(2,1)} %bitcast.85) | data formatting | bytes 8847360 | tf_op jit(solution)/shard_map/reshape.13
  274.1 16.1 %convert_bitcast_fusion = bf16[12,1,360,512]{3,2,0,1:T(8,128)(2,1)} fusion(f32[360,512]{1,0:T(8,128)S(1)} %bitcast.92, bf16[12,360,512]{2,1,0:T(8,128)(2,1)} %reshape.193, f32[512]{0:T(512)S(1)} %fusion.59, s32[512]{0:T(512)S(1)} %multiply_add_fusion), kind=kOutput, calls=%fused_computation.33 | convolution fusion | flops 4544872448 | bytes 9588736 | tf_op jit(solution)/shard_map/alkn,yn->alky/dot_general | solution.py:89
  290.2 8.9 %copy.42 = bf16[12,1,360,512]{2,0,1,3:T(8,128)(2,1)} copy(bf16[12,1,360,512]{3,2,0,1:T(8,128)(2,1)} %convert_bitcast_fusion) | data formatting | bytes 8847360 | tf_op jit(solution)/shard_map/convert_element_type | solution.py:91
  299.2 5.2 %all-to-all-start.3 = ((bf16[12,1,360,512]{2,0,1,3:T(8,128)(2,1)}), bf16[12,1,360,512]{2,0,1,3:T(8,128)(2,1)}, u32[]{:S(2)}, u32[]{:S(2)}) async-start(bf16[12,1,360,512]{2,0,1,3:T(8,128)(2,1)} %copy.42), calls=%async_computation.3 | async-start | bytes 12582912 | tf_op jit(solution)/shard_map/all_to_all | solution.py:92
  304.5 6.4 %copy.34 = f32[12,4,360,128]{3,2,1,0:T(8,128)} copy(bf16[12,4,360,128]{3,2,0,1:T(8,128)(2,1)} %all-to-all-done) | data formatting | bytes 13271040 | tf_op jit(solution)/shard_map/convert_element_type | solution.py:94
  310.9 62.9 %all-to-all-done.3 = bf16[12,1,360,512]{2,0,1,3:T(8,128)(2,1)} async-done(((bf16[12,1,360,512]{2,0,1,3:T(8,128)(2,1)}), bf16[12,1,360,512]{2,0,1,3:T(8,128)(2,1)}, u32[]{:S(2)}, u32[]{:S(2)}) %all-to-all-start.3) | async-done | bytes 4423712 | tf_op jit(solution)/shard_map/all_to_all | solution.py:92
  373.8 8.8 %copy.43 = bf16[12,1,360,4,128]{4,2,3,0,1:T(8,128)(2,1)} copy(bf16[12,1,360,4,128]{2,0,4,3,1:T(8,128)(2,1)} %bitcast.15) | data formatting | bytes 8847360 | tf_op jit(solution)/shard_map/all_to_all | solution.py:92
  382.5 46.6 %fusion.15 = f32[1440,128]{1,0:T(8,128)} fusion(f32[12,4,360,128]{3,2,1,0:T(8,128)} %copy.34, bf16[12,1440,128]{2,1,0:T(8,128)(2,1)} %bitcast.87, f32[1440]{0:T(1024)S(1)} %fusion.58, s32[1440]{0:T(1024)S(1)} %add_select_fusion.2, pred[1440]{0:T(1024)(128)(4,1)S(1)} %iota_compare_fusion.4), kind=kOutput, calls=%fused_computation.21 | convolution fusion | flops 6399221760 | bytes 14021280 | tf_op jit(solution)/shard_map/alky,xk->alxy/dot_general | solution.py:93
  429.1 19.2 %all-reduce.2.cloned.1.call-done = f32[1,1440,128]{2,0,1:T(1,128)} async-done(((f32[1,1440,128]{2,0,1:T(1,128)}), f32[1,1440,128]{2,0,1:T(1,128)}) %all-reduce.2.cloned.1.call-update) | async-done | bytes 737296 | tf_op jit(solution)/shard_map/psum | solution.py:95
  448.3 24.4 %all_to_all.60 = f32[1,1440,128]{2,0,1:T(1,128)S(1)} all-to-all(f32[1,1440,128]{2,0,1:T(1,128)} %all-reduce.2.cloned.1.call-done), channel_id=1, replica_groups=mesh['lat'=4,'lon'=4,'mem'=2] {'lon'}, dimensions={1} | all-to-all | bytes 1474560 | tf_op jit(solution)/shard_map/all_to_all | solution.py:96
  472.7 1.5 broadcast_multiply_fusion.1
  (49 shorter events, 1.5 us)
Async XLA Ops:
  11.1 6.5 %copy-start.2 = (s32[64,128]{1,0:T(8,128)S(1)}, s32[64,128]{1,0:T(8,128)}, u32[]{:S(2)}) copy-start(s32[64,128]{1,0:T(8,128)} %param.10) | copy-start | bytes 98308
  11.1 6.5 %copy-start = (s32[64,128]{1,0:T(8,128)S(1)}, s32[64,128]{1,0:T(8,128)}, u32[]{:S(2)}) copy-start(s32[64,128]{1,0:T(8,128)} %param.11) | copy-start | bytes 98308
  11.1 6.5 %copy-start.1 = (s32[64,128]{1,0:T(8,128)S(1)}, s32[64,128]{1,0:T(8,128)}, u32[]{:S(2)}) copy-start(s32[64,128]{1,0:T(8,128)} %param.12) | copy-start | bytes 98308
  11.1 6.6 %copy-start.3 = (f32[64,128]{1,0:T(8,128)S(1)}, f32[64,128]{1,0:T(8,128)}, u32[]{:S(2)}) copy-start(f32[64,128]{1,0:T(8,128)} %param.13) | copy-start | bytes 98308
  11.1 104.9 %all-to-all-start = ((bf16[12,4,360,128]{3,2,0,1:T(8,128)(2,1)}), bf16[12,4,360,128]{3,2,0,1:T(8,128)(2,1)}, u32[]{:S(2)}, u32[]{:S(2)}) async-start(bf16[12,4,360,128]{3,2,0,1:T(8,128)(2,1)} %copy.33), calls=%async_computation | async-start | bytes 8847360 | tf_op jit(solution)/shard_map/all_to_all | solution.py:78
  116.0 47.6 %all-to-all-start.1 = ((bf16[1,4,360,128]{3,2,0,1:T(8,128)(2,1)}), bf16[1,4,360,128]{3,2,0,1:T(8,128)(2,1)S(1)}, u32[]{:S(2)}, u32[]{:S(2)}) async-start(bf16[1,4,360,128]{3,2,0,1:T(8,128)(2,1)} %bitcast.6), calls=%async_computation.1 | async-start | bytes 737280 | tf_op jit(solution)/shard_map/all_to_all | solution.py:79
  163.6 3.6 copy-start.5
  187.1 70.2 %all-to-all-start.2 = ((bf16[12,1,1440,128]{3,0,1,2:T(8,128)(2,1)}), bf16[12,1,1440,128]{3,0,1,2:T(8,128)(2,1)}, u32[]{:S(2)}, u32[]{:S(2)}) async-start(bf16[12,1,1440,128]{3,0,1,2:T(8,128)(2,1)} %copy.40), calls=%async_computation.2 | async-start | bytes 11796480 | tf_op jit(solution)/shard_map/all_to_all | solution.py:84
  265.5 8.6 %copy-start.4 = (f32[1,360,512]{2,1,0:T(8,128)S(1)}, f32[1,360,512]{2,1,0:T(8,128)}, u32[]{:S(2)}) copy-start(f32[1,360,512]{2,1,0:T(8,128)} %param.9) | copy-start | bytes 2211844
  299.2 74.6 %all-to-all-start.3 = ((bf16[12,1,360,512]{2,0,1,3:T(8,128)(2,1)}), bf16[12,1,360,512]{2,0,1,3:T(8,128)(2,1)}, u32[]{:S(2)}, u32[]{:S(2)}) async-start(bf16[12,1,360,512]{2,0,1,3:T(8,128)(2,1)} %copy.42), calls=%async_computation.3 | async-start | bytes 12582912 | tf_op jit(solution)/shard_map/all_to_all | solution.py:92
  304.4 143.9 %all-reduce.2.cloned.1.call-start = ((), (), s32[]{:S(2)}) async-start(), calls=%async_computation.5 | async-start | bytes 1474560 | tf_op jit(solution)/shard_map/psum | solution.py:95
Sparse Core Ops, SparseCore 0:
  429.2 19.0 all-reduce.1
where the time goes:
time: 487 us; the launch traced here: 481 us
  waiting for transfers between devices  215 us (44%)
  matrix products  96 us (20%)
  local copies, waits for them, and re-layouts  66.3 us (14%)
  other arithmetic  44.8 us (9%)
  blocking collectives  24.4 us (5%)
  starting transfers between devices  20.9 us (4%)
  between operations  13.8 us (3%)
    all_to_all x1, waiting for transfers between devices, local(): lax.all_to_all(anomalies, 'lon', split_axis=1, concat_axis=2, tiled=True)  67.8 us
    all_to_all x1, waiting for transfers between devices, local(): lax.all_to_all(zonal_coef, 'lat', split_axis=2, concat_axis=3, tiled=True)  65 us
    all_to_all x1, waiting for transfers between devices, local(): lax.all_to_all(filtered, 'lat', split_axis=3, concat_axis=2, tiled=True)  62.9 us
    dot_general x1, matrix products, local(): jnp.einsum('alky,xk->alxy', inverse, lon_table, preferred_element_type=jn...  46.6 us
    dot_general x1, other arithmetic, local(): jnp.einsum('alxy,xk->alky', fields * innov_cols, lon_table, preferred_ele...  39 us
    dot_general x4, matrix products, add_block(): jnp.einsum('ok,oz->kz', left_hot, weighted_rows, preferred_element_type=j...  25.7 us
    all_to_all x1, blocking collectives, local(): lax.all_to_all(merged, 'lon', split_axis=1, concat_axis=0, tiled=True)  24.4 us
    psum x1, waiting for transfers between devices, local(): merged = lax.psum(local_sum, 'mem')  19.2 us
  transfers between devices with their start and end apart: 5, of which 4 were waited for; matrix products, arithmetic and copies ran while one was open for 17% of the time, Pallas kernels for 0%

commit v1 on v0

--- a/solution.py
+++ b/solution.py
@@ -5,19 +5,30 @@
 from jax import lax
 from jax.sharding import PartitionSpec as P
 
+def lon_basis(length):
+    nyquist = length // 2
+    inner = next(size for size in range(32, 0, -1) if length % size == 0)
+    outer = length // inner
+    coef_idx = jnp.arange(length, dtype=jnp.int32)
+    wavenum = jnp.where(coef_idx <= nyquist, coef_idx, coef_idx - nyquist)
+    step = 2.0 * math.pi / length
 
-def lon_basis(length):
-    grid_idx = jnp.arange(length, dtype=jnp.int32)[:, None]
-    coef_idx = jnp.arange(length, dtype=jnp.int32)[None, :]
-    nyquist = length // 2
-    wavenum = jnp.where(coef_idx <= nyquist, coef_idx, coef_idx - nyquist)
-    phase_idx = grid_idx * wavenum % length
-    angles = phase_idx.astype(jnp.float32) * (2.0 * math.pi / length)
+    def angles(points):
+        return (points[:, None] * wavenum[None, :] % length).astype(jnp.float32) * step
+
+    coarse = angles(jnp.arange(outer, dtype=jnp.int32) * inner)
+    fine = angles(jnp.arange(inner, dtype=jnp.int32))
     scales = jnp.where(
         (coef_idx == 0) | (coef_idx == nyquist), 1.0 / math.sqrt(length), math.sqrt(2.0 / length)
     )
-    basis = jnp.where(coef_idx <= nyquist, jnp.cos(angles), jnp.sin(angles)) * scales
-    return basis.astype(jnp.bfloat16)
+    is_cos = (coef_idx <= nyquist)[None, :]
+    coarse_cos, coarse_sin = jnp.cos(coarse) * scales, jnp.sin(coarse) * scales
+    fine_cos, fine_sin = jnp.cos(fine), jnp.sin(fine)
+    first = jnp.where(is_cos, coarse_cos, coarse_sin)
+    second = jnp.where(is_cos, -coarse_sin, coarse_cos)
+    first, second, fine_cos, fine_sin = lax.optimization_barrier((first, second, fine_cos, fine_sin))
+    basis = first[:, None, :] * fine_cos[None] + second[:, None, :] * fine_sin[None]
+    return basis.reshape(length, length).astype(jnp.bfloat16)
 
 
 def lat_basis(length):
@@ -61,8 +72,20 @@
 
 def local(anomalies, taper, obs_row, obs_col, obs_level, obs_value):
     member_count, level_count, col_count, row_count = anomalies.shape
-    lon_total = col_count * lax.axis_size("lon")
-    lat_total = row_count * lax.axis_size("lat")
+    lon_size, lat_size = lax.axis_size("lon"), lax.axis_size("lat")
+    lon_total = col_count * lon_size
+    lat_total = row_count * lat_size
+    ensemble = member_count * lax.axis_size("mem")
+    own_members = member_count // lat_size
+    everyone = ("lat", "lon")
+    grouped = anomalies.reshape(lat_size, own_members, lon_size, col_count, row_count)
+    fields = [
+        lax.all_to_all(
+            grouped[:, turn].reshape(lat_size * lon_size, col_count, row_count),
+            everyone, split_axis=0, concat_axis=0, tiled=True,
+        )
+        for turn in range(own_members)
+    ]
     row_start = lax.axis_index("lat") * row_count
     col_start = lax.axis_index("lon") * col_count
     cell_keys = (obs_level * col_count + (obs_col - col_start)).reshape(-1)
@@ -71,30 +94,31 @@
         cell_keys, row_local, obs_value.reshape(-1), level_count * col_count, row_count
     )
     innovation = innovation.reshape(level_count, col_count, row_count).astype(jnp.bfloat16)
+    innov_cols = lax.all_to_all(innovation, "lon", split_axis=0, concat_axis=0, tiled=True)
+    innov_all = lax.all_gather(innov_cols.reshape(lon_total, row_count), "lat")
+    taper_all = lax.all_gather(
+        taper[0].astype(jnp.bfloat16), "lat", axis=0, tiled=True
+    ).astype(jnp.float32)
     lon_table = lon_basis(lon_total)
     lat_table = lat_basis(lat_total)
-    ensemble = member_count * lax.axis_size("mem")
-    fields, innov_cols = (
-        lax.all_to_all(anomalies, "lon", split_axis=1, concat_axis=2, tiled=True),
-        lax.all_to_all(innovation[None], "lon", split_axis=1, concat_axis=2, tiled=True),
-    )
-    zonal_coef = jnp.einsum(
-        "alxy,xk->alky", fields * innov_cols, lon_table, preferred_element_type=jnp.float32
-    ).astype(jnp.bfloat16)
-    modal_zonal_coef = lax.all_to_all(zonal_coef, "lat", split_axis=2, concat_axis=3, tiled=True)
-    spectrum = jnp.einsum(
-        "alky,yn->alkn", modal_zonal_coef, lat_table, preferred_element_type=jnp.float32
-    )
-    tapered = (spectrum * taper[None]).astype(jnp.bfloat16)
-    filtered = jnp.einsum(
-        "alkn,yn->alky", tapered, lat_table, preferred_element_type=jnp.float32
-    ).astype(jnp.bfloat16)
-    inverse = lax.all_to_all(filtered, "lat", split_axis=3, concat_axis=2, tiled=True)
-    localized = jnp.einsum("alky,xk->alxy", inverse, lon_table, preferred_element_type=jnp.float32)
-    local_sum = jnp.sum(fields.astype(jnp.float32) * localized, axis=0)
-    merged = lax.psum(local_sum, "mem")
-    summed = lax.all_to_all(merged, "lon", split_axis=1, concat_axis=0, tiled=True)
-    return summed / (ensemble - 1)
+    total = jnp.zeros((lat_size, lon_total, row_count), jnp.float32)
+    for turn in range(own_members):
+        field = fields[turn].reshape(lat_size, lon_total, row_count)
+        zonal = jnp.einsum(
+            "ixy,xk->kiy", field * innov_all, lon_table, preferred_element_type=jnp.float32
+        ).astype(jnp.bfloat16).reshape(lon_total, lat_total)
+        spectrum = jnp.einsum("ky,yn->kn", zonal, lat_table, preferred_element_type=jnp.float32)
+        tapered = (spectrum * taper_all).astype(jnp.bfloat16)
+        inverse = jnp.einsum(
+            "kn,yn->ky", tapered, lat_table, preferred_element_type=jnp.float32
+        ).astype(jnp.bfloat16).reshape(lon_total, lat_size, row_count)
+        localized = jnp.einsum("kiy,xk->ixy", inverse, lon_table, preferred_element_type=jnp.float32)
+        total = total + field.astype(jnp.float32) * localized
+    parts = lax.all_to_all(total.astype(jnp.bfloat16), "lat", split_axis=0, concat_axis=0, tiled=True)
+    merged = lax.psum(jnp.sum(parts.astype(jnp.float32), axis=0), "mem")
+    blocks = merged.reshape(lon_size, col_count, row_count) / (ensemble - 1)
+    summed = lax.all_to_all(blocks.astype(jnp.bfloat16), "lon", split_axis=0, concat_axis=0, tiled=True)
+    return summed.astype(jnp.float32)
 
 
 def solution(mesh):

time: 487 us -> 312 us (0.64)
  waiting for transfers between devices: 215 us -> 86.9 us
  local copies, waits for them, and re-layouts: 66.3 us -> 10.4 us
  blocking collectives: 24.4 us -> 77.1 us
  other arithmetic: 44.8 us -> 16 us
  matrix products: 96 us -> 86.8 us
  starting transfers between devices: 20.9 us -> 15 us
    all_to_all x4 -> x3, waiting for transfers between devices: 196 us -> 69.6 us  [the longest x2 62.7 us: local(): lax.all_to_all(grouped[:, turn].reshape(lat_size * lon_size, col_count, r...]
    all_to_all x1 -> x3, blocking collectives: 24.4 us -> 77.1 us  [the longest x1 40.1 us: local(): lax.all_to_all(grouped[:, turn].reshape(lat_size * lon_size, col_count, r...]
    dot_general x1 -> x0, other arithmetic: 39 us -> none  [local(): jnp.einsum('alxy,xk->alky', fields * innov_cols, lon_table, preferred_ele...]
    convert_element_type x3 -> x0, local copies, waits for them, and re-layouts: 27.7 us -> none  [the longest x1 12.3 us: local(): zonal_coef = jnp.einsum('alxy,xk->alky', fields * innov_cols, lon_table,...]
    all_to_all x3 -> x0, local copies, waits for them, and re-layouts: 21.6 us -> none  [the longest x1 8.75 us: local(): lax.all_to_all(filtered, 'lat', split_axis=3, concat_axis=2, tiled=True)]
    another operation x1 -> x0, local copies, waits for them, and re-layouts: 8.6 us -> none
    convert_element_type x0 -> x4, other arithmetic: none -> 7.51 us  [the longest x1 3.53 us: lon_basis(): return basis.reshape(length, length).astype(jnp.bfloat16)]
    dot_general x4, matrix products: 25.7 us -> 18.3 us  [add_block(): jnp.einsum('ok,oz->kz', left_hot, weighted_rows, preferred_element_type=j...]
  transfers between devices with their start and end apart: 5 -> 6, of which waited for: 4 -> 4; matrix products, arithmetic and copies ran while one was open for 17% -> 8% of each run, Pallas kernels for 0% -> 0%
where the time goes in v1:
time: 312 us; the launch traced here: 306 us
  waiting for transfers between devices  86.9 us (28%)
  matrix products  86.8 us (28%)
  blocking collectives  77.1 us (25%)
  other arithmetic  16 us (5%)
  starting transfers between devices  15 us (5%)
  between operations  13.7 us (4%)
  local copies, waits for them, and re-layouts  10.4 us (3%)
    all_to_all x2, waiting for transfers between devices, local(): lax.all_to_all(grouped[:, turn].reshape(lat_size * lon_size, col_count, r...  62.7 us
    all_to_all x1, blocking collectives, local(): lax.all_to_all(grouped[:, turn].reshape(lat_size * lon_size, col_count, r...  40.1 us
    dot_general x3, matrix products, local(): jnp.einsum('kn,yn->ky', tapered, lat_table, preferred_element_type=jnp.fl...  36.3 us
    dot_general x3, matrix products, local(): jnp.einsum('kiy,xk->ixy', inverse, lon_table, preferred_element_type=jnp....  21.3 us
    all_to_all x1, blocking collectives, local(): lax.all_to_all(total.astype(jnp.bfloat16), 'lat', split_axis=0, concat_ax...  20.8 us
    dot_general x4, matrix products, add_block(): jnp.einsum('ok,oz->kz', left_hot, weighted_rows, preferred_element_type=j...  18.3 us
    psum x1, waiting for transfers between devices, local(): merged = lax.psum(jnp.sum(parts.astype(jnp.float32), axis=0), 'mem')  16.6 us
    all_to_all x1, blocking collectives, local(): lax.all_to_all(blocks.astype(jnp.bfloat16), 'lon', split_axis=0, concat_a...  16.3 us
  transfers between devices with their start and end apart: 6, of which 4 were waited for; matrix products, arithmetic and copies ran while one was open for 8% of the time, Pallas kernels for 0%

profile of v1, /device:TPU:0, one launch (start us, length us, event | category | flops | bytes accessed | tf_op | source)
XLA Modules:
  0.0 306.2 jit_solution(6583486104414878671)
XLA Ops:
  8.9 19.9 %while.11 = (s32[]{:T(128)}, f32[1440,384]{1,0:T(8,128)S(1)}, s32[4,2048]{1,0:T(4,128)S(1)}, f32[4,2048]{1,0:T(4,128)S(1)}, s32[4,2048]{1,0:T(4,128)S(1)}, /*index=5*/s32[]{:T(128)}, s32[]{:T(128)}) while((s32[]{:T(128)}, f32[1440,384]{1,0:T(8,128)S(1)}, s32[4,2048]{1,0:T(4,128)S(1)}, f32[4,2048]{1,0:T(4,128)S(1)}, ...), condition=%wide.region_1.2_spmd.clone, body=%wide.region_0.1_spmd.clone.sunk | while | flops 2273290240 | bytes 8728683 | solution.py:69
  9.3 4.6 %fusion.121 = f32[1440,384]{1,0:T(8,128)S(1)} fusion(bf16[2048,384]{0,1:T(8,128)(2,1)S(1)} %bitcast.121, s32[2048]{0:T(1024)S(1)} %bitcast.140, f32[1440,384]{1,0:T(8,128)S(1)} %get-tuple-element.144, pred[]{:T(512)S(6)} %compare.4), kind=kOutput, calls=%fused_computation.6.clone.1 | convolution fusion | flops 2271928320 | bytes 6004737 | tf_op jit(solution)/shard_map/while/body/eval_jaxpr/ok,oz->kz/dot_general | solution.py:65
  14.3 4.6 %fusion.121 = f32[1440,384]{1,0:T(8,128)S(1)} fusion(bf16[2048,384]{0,1:T(8,128)(2,1)S(1)} %bitcast.121, s32[2048]{0:T(1024)S(1)} %bitcast.140, f32[1440,384]{1,0:T(8,128)S(1)} %get-tuple-element.144, pred[]{:T(512)S(6)} %compare.4), kind=kOutput, calls=%fused_computation.6.clone.1 | convolution fusion | flops 2271928320 | bytes 6004737 | tf_op jit(solution)/shard_map/while/body/eval_jaxpr/ok,oz->kz/dot_general | solution.py:65
  19.3 4.6 %fusion.121 = f32[1440,384]{1,0:T(8,128)S(1)} fusion(bf16[2048,384]{0,1:T(8,128)(2,1)S(1)} %bitcast.121, s32[2048]{0:T(1024)S(1)} %bitcast.140, f32[1440,384]{1,0:T(8,128)S(1)} %get-tuple-element.144, pred[]{:T(512)S(6)} %compare.4), kind=kOutput, calls=%fused_computation.6.clone.1 | convolution fusion | flops 2271928320 | bytes 6004737 | tf_op jit(solution)/shard_map/while/body/eval_jaxpr/ok,oz->kz/dot_general | solution.py:65
  24.2 4.6 %fusion.121 = f32[1440,384]{1,0:T(8,128)S(1)} fusion(bf16[2048,384]{0,1:T(8,128)(2,1)S(1)} %bitcast.121, s32[2048]{0:T(1024)S(1)} %bitcast.140, f32[1440,384]{1,0:T(8,128)S(1)} %get-tuple-element.144, pred[]{:T(512)S(6)} %compare.4), kind=kOutput, calls=%fused_computation.6.clone.1 | convolution fusion | flops 2271928320 | bytes 6004737 | tf_op jit(solution)/shard_map/while/body/eval_jaxpr/ok,oz->kz/dot_general | solution.py:65
  28.8 1.4 copy-done.1
  30.2 2.0 copy.45
  33.4 6.3 %all-to-all-start.1 = ((bf16[4,360,128]{2,1,0:T(8,128)(2,1)}), bf16[4,360,128]{2,1,0:T(8,128)(2,1)S(1)}, u32[]{:S(2)}, u32[]{:S(2)}) async-start(bf16[4,360,128]{2,1,0:T(8,128)(2,1)} %bitcast.7), calls=%async_computation.1 | async-start | bytes 737280 | tf_op jit(solution)/shard_map/all_to_all | solution.py:97
  39.7 4.2 %fusion.101 = (bf16[4,1,4,360,128]{4,3,2,1,0:T(8,128)(2,1)}, bf16[4,1,4,360,128]{4,3,2,1,0:T(8,128)(2,1)S(1)}, bf16[4,1,4,360,128]{4,3,2,1,0:T(8,128)(2,1)}) fusion(bf16[4,3,4,360,128]{4,3,2,1,0:T(8,128)(2,1)} %bitcast.130), kind=kLoop, calls=%fused_computation.118 | loop fusion | bytes 8847360 | tf_op jit(solution)/shard_map/slice | solution.py:84
  44.0 6.9 %all-to-all-done.1 = bf16[4,360,128]{2,1,0:T(8,128)(2,1)S(1)} async-done(((bf16[4,360,128]{2,1,0:T(8,128)(2,1)}), bf16[4,360,128]{2,1,0:T(8,128)(2,1)S(1)}, u32[]{:S(2)}, u32[]{:S(2)}) %all-to-all-start.1) | async-done | bytes 368672 | tf_op jit(solution)/shard_map/all_to_all | solution.py:97
  50.9 40.1 %all_to_all.30 = bf16[16,360,128]{2,1,0:T(8,128)(2,1)S(1)} all-to-all(bf16[16,360,128]{2,1,0:T(8,128)(2,1)S(1)} %bitcast.129), channel_id=1, replica_groups=mesh['lat'=4,'lon'=4,'mem'=2] {'lat','lon'}, dimensions={0} | all-to-all | bytes 2949120 | tf_op jit(solution)/shard_map/all_to_all | solution.py:83
  91.0 3.7 %all-to-all-start = ((bf16[16,360,128]{2,1,0:T(8,128)(2,1)}), bf16[16,360,128]{2,1,0:T(8,128)(2,1)S(1)}, u32[]{:S(2)}, u32[]{:S(2)}) async-start(bf16[16,360,128]{2,1,0:T(8,128)(2,1)} %bitcast.128), calls=%async_computation | async-start | bytes 2949120 | tf_op jit(solution)/shard_map/all_to_all | solution.py:83
  95.4 35.2 %all-to-all-done = bf16[16,360,128]{2,1,0:T(8,128)(2,1)S(1)} async-done(((bf16[16,360,128]{2,1,0:T(8,128)(2,1)}), bf16[16,360,128]{2,1,0:T(8,128)(2,1)S(1)}, u32[]{:S(2)}, u32[]{:S(2)}) %all-to-all-start) | async-done | bytes 1474592 | tf_op jit(solution)/shard_map/all_to_all | solution.py:83
  130.6 4.4 %all-to-all-start.2 = ((bf16[16,360,128]{2,1,0:T(8,128)(2,1)}), bf16[16,360,128]{2,1,0:T(8,128)(2,1)}, u32[]{:S(2)}, u32[]{:S(2)}) async-start(bf16[16,360,128]{2,1,0:T(8,128)(2,1)} %bitcast.127), calls=%async_computation.2 | async-start | bytes 2949120 | tf_op jit(solution)/shard_map/all_to_all | solution.py:83
  135.1 1.9 convert_element_type.207
  138.4 1.3 negate_select_fusion.2
  139.8 3.5 %add_convert_fusion = bf16[45,32,1440]{2,1,0:T(8,128)(2,1)} fusion(f32[32,1440]{1,0:T(8,128)S(1)} %get-tuple-element.49, f32[45,1440]{1,0:T(8,128)S(1)} %get-tuple-element.48, f32[32,1440]{1,0:T(8,128)S(1)} %get-tuple-element.47, f32[45,1440]{1,0:T(8,128)S(1)} %get-tuple-element.46), kind=kLoop, calls=%fused_computation.17 | loop fusion | flops 8294400 | bytes 5034240 | tf_op jit(solution)/shard_map/convert_element_type | solution.py:31
  143.3 27.5 %all-to-all-done.2 = bf16[16,360,128]{2,1,0:T(8,128)(2,1)} async-done(((bf16[16,360,128]{2,1,0:T(8,128)(2,1)}), bf16[16,360,128]{2,1,0:T(8,128)(2,1)}, u32[]{:S(2)}, u32[]{:S(2)}) %all-to-all-start.2) | async-done | bytes 1474592 | tf_op jit(solution)/shard_map/all_to_all | solution.py:83
  170.8 2.3 bitcast_multiply_fusion.2
  174.0 3.6 %fusion.37 = bf16[4,180,8,128]{3,2,1,0:T(8,128)(2,1)} fusion(bf16[1440,1440,1]{1,0,2:T(8,128)(2,1)S(1)} %bitcast.134, bf16[4,1440,128]{2,1,0:T(8,128)(2,1)S(1)} %get-tuple-element.90), kind=kOutput, calls=%fused_computation.61 | convolution fusion | flops 2124103680 | bytes 7096320 | tf_op jit(solution)/shard_map/ixy,xk->kiy/dot_general | solution.py:107
  177.6 3.6 %fusion.39 = bf16[4,180,8,128]{3,2,1,0:T(8,128)(2,1)} fusion(bf16[1440,1440,1]{1,0,2:T(8,128)(2,1)S(1)} %bitcast.135, bf16[4,1440,128]{2,1,0:T(8,128)(2,1)S(1)} %get-tuple-element.91), kind=kOutput, calls=%fused_computation.63 | convolution fusion | flops 2124103680 | bytes 7096320 | tf_op jit(solution)/shard_map/ixy,xk->kiy/dot_general | solution.py:107
  181.2 3.7 %fusion.38 = bf16[4,180,8,128]{3,2,1,0:T(8,128)(2,1)} fusion(bf16[1440,1440,1]{1,0,2:T(8,128)(2,1)S(1)} %bitcast.136, bf16[4,1440,128]{2,1,0:T(8,128)(2,1)S(1)} %get-tuple-element.92), kind=kOutput, calls=%fused_computation.62 | convolution fusion | flops 2124103680 | bytes 7096320 | tf_op jit(solution)/shard_map/ixy,xk->kiy/dot_general | solution.py:107
  184.9 12.2 %fusion.36 = bf16[180,4,8,128]{3,2,1,0:T(8,128)(2,1)} fusion(bf16[4,180,8,128]{3,2,1,0:T(8,128)(2,1)} %fusion.39, bf16[1,1440,512]{2,1,0:T(8,128)(2,1)} %all-gather.6.cloned.1.call-done, f32[512]{0:T(512)S(1)} %fusion.76, s32[512]{0:T(512)S(1)} %multiply_add_fusion), kind=kOutput, calls=%fused_computation.60 | convolution fusion | flops 1521287168 | bytes 4427776 | tf_op jit(solution)/shard_map/kn,yn->ky/dot_general | solution.py:112
  197.1 6.8 %fusion.13 = f32[4,1440,128]{2,1,0:T(8,128)} fusion(bf16[1440,1440,1]{1,0,2:T(8,128)(2,1)} %bitcast.131, bf16[4,1440,128]{2,1,0:T(8,128)(2,1)S(1)} %bitcast.126, bf16[180,4,8,128]{3,2,1,0:T(8,128)(2,1)} %fusion.36), kind=kOutput, calls=%fused_computation.22 | convolution fusion | flops 2124840960 | bytes 10045440 | tf_op jit(solution)/shard_map/kiy,xk->ixy/dot_general | solution.py:115
  203.9 12.3 %fusion.35 = bf16[180,4,8,128]{3,2,1,0:T(8,128)(2,1)} fusion(bf16[4,180,8,128]{3,2,1,0:T(8,128)(2,1)} %fusion.38, bf16[1,1440,512]{2,1,0:T(8,128)(2,1)} %all-gather.6.cloned.1.call-done, f32[512]{0:T(512)S(1)} %fusion.76, s32[512]{0:T(512)S(1)} %multiply_add_fusion), kind=kOutput, calls=%fused_computation.59 | convolution fusion | flops 1521287168 | bytes 4427776 | tf_op jit(solution)/shard_map/kn,yn->ky/dot_general | solution.py:112
  216.1 7.3 %fusion.14 = f32[4,1440,128]{2,1,0:T(8,128)} fusion(bf16[1440,1440,1]{1,0,2:T(8,128)(2,1)} %bitcast.132, bf16[4,1440,128]{2,1,0:T(8,128)(2,1)} %bitcast.12, bf16[180,4,8,128]{3,2,1,0:T(8,128)(2,1)} %fusion.35), kind=kOutput, calls=%fused_computation.24 | convolution fusion | flops 2124840960 | bytes 10045440 | tf_op jit(solution)/shard_map/kiy,xk->ixy/dot_general | solution.py:115
  223.5 11.8 %fusion.34 = bf16[180,4,8,128]{3,2,1,0:T(8,128)(2,1)} fusion(bf16[4,180,8,128]{3,2,1,0:T(8,128)(2,1)} %fusion.37, bf16[1,1440,512]{2,1,0:T(8,128)(2,1)S(1)} %copy-done.3, f32[512]{0:T(512)S(1)} %fusion.76, s32[512]{0:T(512)S(1)} %multiply_add_fusion), kind=kOutput, calls=%fused_computation.58 | convolution fusion | flops 1521287168 | bytes 4427776 | tf_op jit(solution)/shard_map/kn,yn->ky/dot_general | solution.py:112
  235.3 7.2 %fusion.18 = bf16[4,1440,128]{2,1,0:T(8,128)(2,1)S(1)} fusion(f32[4,1440,128]{2,1,0:T(8,128)} %fusion.13, f32[4,1440,128]{2,1,0:T(8,128)} %fusion.14, bf16[1440,1440,1]{1,0,2:T(8,128)(2,1)} %bitcast.133, bf16[4,1440,128]{2,1,0:T(8,128)(2,1)S(1)} %bitcast.124, bf16[180,4,8,128]{3,2,1,0:T(8,128)(2,1)} %fusion.34), kind=kOutput, calls=%fused_computation.32 | convolution fusion | flops 2127052800 | bytes 14469120 | tf_op jit(solution)/shard_map/kiy,xk->ixy/dot_general | solution.py:115
  242.4 20.8 %all_to_all.31 = bf16[4,1440,128]{2,1,0:T(8,128)(2,1)S(1)} all-to-all(bf16[4,1440,128]{2,1,0:T(8,128)(2,1)S(1)} %fusion.18), channel_id=1, replica_groups=mesh['lat'=4,'lon'=4,'mem'=2] {'lat'}, dimensions={0} | all-to-all | bytes 2949120 | tf_op jit(solution)/shard_map/all_to_all | solution.py:117
  264.3 16.6 %all-reduce.2.cloned.1.call-done = f32[1440,128]{1,0:T(8,128)} async-done(((f32[1440,128]{1,0:T(8,128)}), f32[1440,128]{1,0:T(8,128)}) %all-reduce.2.cloned.1.call-update) | async-done | bytes 737296 | tf_op jit(solution)/shard_map/psum | solution.py:118
  280.9 1.2 multiply_convert_fusion
  282.1 16.3 %all_to_all.32 = bf16[4,360,128]{2,1,0:T(8,128)(2,1)S(1)} all-to-all(bf16[4,360,128]{2,1,0:T(8,128)(2,1)S(1)} %bitcast.138), channel_id=1, replica_groups=mesh['lat'=4,'lon'=4,'mem'=2] {'lon'}, dimensions={0} | all-to-all | bytes 737280 | tf_op jit(solution)/shard_map/all_to_all | solution.py:120
  (56 shorter events, 9.8 us)
Async XLA Ops:
  28.8 1.4 copy-start.1
  33.4 17.5 %all-to-all-start.1 = ((bf16[4,360,128]{2,1,0:T(8,128)(2,1)}), bf16[4,360,128]{2,1,0:T(8,128)(2,1)S(1)}, u32[]{:S(2)}, u32[]{:S(2)}) async-start(bf16[4,360,128]{2,1,0:T(8,128)(2,1)} %bitcast.7), calls=%async_computation.1 | async-start | bytes 737280 | tf_op jit(solution)/shard_map/all_to_all | solution.py:97
  50.9 40.1 %copy-start.2 = (bf16[4,360,128]{2,1,0:T(8,128)(2,1)}, bf16[4,360,128]{2,1,0:T(8,128)(2,1)S(1)}, u32[]{:S(2)}) copy-start(bf16[4,360,128]{2,1,0:T(8,128)(2,1)S(1)} %all-to-all-done.1) | copy-start | bytes 1105924
  91.0 39.6 %all-to-all-start = ((bf16[16,360,128]{2,1,0:T(8,128)(2,1)}), bf16[16,360,128]{2,1,0:T(8,128)(2,1)S(1)}, u32[]{:S(2)}, u32[]{:S(2)}) async-start(bf16[16,360,128]{2,1,0:T(8,128)(2,1)} %bitcast.128), calls=%async_computation | async-start | bytes 2949120 | tf_op jit(solution)/shard_map/all_to_all | solution.py:83
  94.7 76.1 %all-gather.4.cloned.1.call-start = ((), (), s32[]{:S(2)}) async-start(), calls=%async_computation.6 | async-start | bytes 1843200 | tf_op jit(solution)/shard_map/all_gather | solution.py:98
  130.6 40.2 %all-to-all-start.2 = ((bf16[16,360,128]{2,1,0:T(8,128)(2,1)}), bf16[16,360,128]{2,1,0:T(8,128)(2,1)}, u32[]{:S(2)}, u32[]{:S(2)}) async-start(bf16[16,360,128]{2,1,0:T(8,128)(2,1)} %bitcast.127), calls=%async_computation.2 | async-start | bytes 2949120 | tf_op jit(solution)/shard_map/all_to_all | solution.py:83
  135.0 49.8 %all-gather.6.cloned.1.call-start = ((), (), s32[]{:S(2)}) async-start(), calls=%async_computation.8 | async-start | bytes 1843200 | tf_op jit(solution)/shard_map/all_gather | solution.py:99
  137.0 143.9 %all-reduce.2.cloned.1.call-start = ((), (), s32[]{:S(2)}) async-start(), calls=%async_computation.7 | async-start | bytes 1474560 | tf_op jit(solution)/shard_map/psum | solution.py:118
  170.8 3.1 %copy-start = (bf16[45,32,1440]{2,1,0:T(8,128)(2,1)S(1)}, bf16[45,32,1440]{2,1,0:T(8,128)(2,1)}, u32[]{:S(2)}) copy-start(bf16[45,32,1440]{2,1,0:T(8,128)(2,1)} %add_convert_fusion) | copy-start | bytes 12441604
  216.1 7.3 %copy-start.3 = (bf16[1,1440,512]{2,1,0:T(8,128)(2,1)S(1)}, bf16[1,1440,512]{2,1,0:T(8,128)(2,1)}, u32[]{:S(2)}) copy-start(bf16[1,1440,512]{2,1,0:T(8,128)(2,1)} %all-gather.6.cloned.1.call-done) | copy-start | bytes 4423684
Sparse Core Ops, SparseCore 0:
  97.4 50.4 all-gather.3
  149.7 30.4 all-gather.5
  264.4 16.4 all-reduce.1

commit v2 on v1

v2 whole, which is shorter than its diff:
```python
import functools
import math

import jax
import jax.numpy as jnp
from jax import lax
from jax.experimental import pallas as pl
from jax.experimental.pallas import tpu as pltpu
from jax.sharding import PartitionSpec as P

def lon_basis(length):
    nyquist = length // 2
    inner = next(size for size in range(32, 0, -1) if length % size == 0)
    outer = length // inner
    coef_idx = jnp.arange(length, dtype=jnp.int32)
    wavenum = jnp.where(coef_idx <= nyquist, coef_idx, coef_idx - nyquist)
    step = 2.0 * math.pi / length

    def angles(points):
        return (points[:, None] * wavenum[None, :] % length).astype(jnp.float32) * step

    coarse = angles(jnp.arange(outer, dtype=jnp.int32) * inner)
    fine = angles(jnp.arange(inner, dtype=jnp.int32))
    scales = jnp.where(
        (coef_idx == 0) | (coef_idx == nyquist), 1.0 / math.sqrt(length), math.sqrt(2.0 / length)
    )
    is_cos = (coef_idx <= nyquist)[None, :]
    coarse_cos, coarse_sin = jnp.cos(coarse) * scales, jnp.sin(coarse) * scales
    fine_cos, fine_sin = jnp.cos(fine), jnp.sin(fine)
    first = jnp.where(is_cos, coarse_cos, coarse_sin)
    second = jnp.where(is_cos, -coarse_sin, coarse_cos)
    first, second, fine_cos, fine_sin = lax.optimization_barrier((first, second, fine_cos, fine_sin))
    basis = first[:, None, :] * fine_cos[None] + second[:, None, :] * fine_sin[None]
    return basis.reshape(length, length).astype(jnp.bfloat16)


def lat_basis(length):
    grid_idx = jnp.arange(length, dtype=jnp.int32)[:, None]
    mode_idx = jnp.arange(length, dtype=jnp.int32)[None, :]
    phase_idx = mode_idx * (2 * grid_idx + 1) % (4 * length)
    angles = phase_idx.astype(jnp.float32) * (math.pi / (2.0 * length))
    scales = jnp.where(mode_idx == 0, 1.0 / math.sqrt(length), math.sqrt(2.0 / length))
    return (jnp.cos(angles) * scales).astype(jnp.bfloat16)


def fused_kernel(
    lat_size, lon_size, own, obs_rows,
    anom, taper, level, column, row, value, lon_fwd, lon_inv, lat_fwd, lat_inv, out,
    fields, table_fwd, table_inv, modes_fwd, modes_inv, taper_all, hits, innov_own, innov_all,
    weighted, inverse, total, partner_part, lat_send, lat_recv, lon_send, lon_recv,
    field_ss, field_rs, local_sem, table_sem, taper_ss, taper_rs, innov_ss, innov_rs,
    gather_ss, gather_rs, mem_sem, lat_ss, lat_rs, lon_ss, lon_rs, pair_sem,
):
    lat, lon, mem = lax.axis_index("lat"), lax.axis_index("lon"), lax.axis_index("mem")
    place_count = lat_size * lon_size
    half = lon_size // 2
    me = lat * lon_size + lon
    col_count, row_count = fields.shape[3:]
    f32, bf16 = jnp.float32, jnp.bfloat16

    def device(lat_idx, lon_idx, mem_idx):
        return {"lat": lat_idx, "lon": lon_idx, "mem": mem_idx}

    def place(offset):
        spot = lax.rem(me + offset, place_count)
        return lax.div(spot, lon_size), lax.rem(spot, lon_size)

    def remote(src, dst, send, recv, target):
        return pltpu.make_async_remote_copy(
            src_ref=src, dst_ref=dst, send_sem=send, recv_sem=recv,
            device_id=target, device_id_type=pl.DeviceIdType.MESH,
        )

    barrier = pltpu.get_barrier_semaphore()

    @pl.loop(1, place_count)
    def _(offset):
        lat_idx, lon_idx = place(offset)
        pl.semaphore_signal(
            barrier, inc=1, device_id=device(lat_idx, lon_idx, mem),
            device_id_type=pl.DeviceIdType.MESH,
        )

    pl.semaphore_signal(
        barrier, inc=1, device_id=device(lat, lon, 1 - mem),
        device_id_type=pl.DeviceIdType.MESH,
    )
    pl.semaphore_wait(barrier, place_count)

    def field_copy(turn, offset):
        lat_idx, lon_idx = place(offset)
        return remote(
            anom.at[lat_idx * own + turn, lon_idx], fields.at[turn, lat, lon],
            field_ss.at[turn, offset], field_rs.at[turn, offset], device(lat_idx, lon_idx, mem),
        )

    def send_fields(turn):
        @pl.loop(1, place_count)
        def _(offset):
            field_copy(turn, offset).start()

    def own_copy(turn):
        return pltpu.make_async_copy(
            anom.at[lat * own + turn, lon], fields.at[turn, lat, lon], local_sem.at[turn]
        )

    send_fields(0)
    taper_copies = [
        remote(
            taper, taper_all.at[lat], taper_ss.at[step], taper_rs.at[step],
            device(lax.rem(lat + step, lat_size), lon, mem),
        )
        for step in range(1, lat_size)
    ]
    table_copies = [
        pltpu.make_async_copy(src, dst, table_sem.at[idx])
        for idx, (src, dst) in enumerate([
            (lon_fwd, table_fwd), (lon_inv, table_inv), (lat_fwd, modes_fwd),
            (lat_inv, modes_inv), (taper, taper_all.at[lat]),
        ])
    ]
    for copy in table_copies:
        copy.start()
    for turn in range(own):
        own_copy(turn).start()

    hits[...] = jnp.zeros_like(hits)
    col_start, row_start = lon * col_count, lat * row_count
    group = 4

    @pl.loop(0, obs_rows // group)
    def _(step):
        def wide(ref):
            return jnp.concatenate([ref[pl.ds(step * group + part, 1), :] for part in range(group)], axis=1)

        keys = wide(level) * col_count + (wide(column) - col_start)
        local_row = wide(row) - row_start
        amount = wide(value)
        width = keys.shape[1]
        high = amount.astype(bf16).astype(f32)
        low = amount - high
        row_hot = lax.broadcasted_iota(jnp.int32, (row_count, width), 0) == local_row
        right = jnp.concatenate(
            [jnp.where(row_hot, high, 0.0).astype(bf16), jnp.where(row_hot, low, 0.0).astype(bf16)], axis=0
        )
        cells = lax.broadcasted_iota(jnp.int32, (col_count, width), 0)
        for lev in range(lon_size):
            left = jnp.where(cells == keys - lev * col_count, 1.0, 0.0).astype(bf16)
            hits[lev] += lax.dot_general(
                left, right, (((1,), (1,)), ((), ())), preferred_element_type=f32
            )

    for lev in range(lon_size):
        innov_own[lev] = (hits[lev, :, :row_count] + hits[lev, :, row_count:]).astype(bf16)
    innov_copies = [
        remote(
            innov_own.at[lax.rem(lon + step, lon_size)], innov_all.at[lat, lon],
            innov_ss.at[step], innov_rs.at[step], device(lat, lax.rem(lon + step, lon_size), mem),
        )
        for step in range(1, lon_size)
    ]
    for copy in innov_copies:
        copy.start()
    innov_local = pltpu.make_async_copy(innov_own.at[lon], innov_all.at[lat, lon], innov_ss.at[0])
    innov_local.start()
    for copy in taper_copies:
        copy.start()
    send_fields(1)
    innov_local.wait()
    for copy in innov_copies:
        copy.wait_recv()
    gather_copies = [
        remote(
            innov_all.at[lat], innov_all.at[lat], gather_ss.at[step], gather_rs.at[step],
            device(lax.rem(lat + step, lat_size), lon, mem),
        )
        for step in range(1, lat_size)
    ]
    for copy in gather_copies:
        copy.start()
    for turn in range(2, own):
        send_fields(turn)
    total[...] = jnp.zeros_like(total)
    for copy in table_copies:
        copy.wait()
    for copy in taper_copies + gather_copies:
        copy.wait_recv()

    @pl.loop(0, own)
    def _(turn):
        own_copy(turn).wait()

        @pl.loop(1, place_count)
        def _(offset):
            field_copy(turn, offset).wait_recv()

        @pl.loop(0, lon_size)
        def _(block):
            for band in range(lat_size):
                product = fields[turn, band, block].astype(f32) * innov_all[band, block].astype(f32)
                weighted[block, :, band * row_count:(band + 1) * row_count] = product.astype(bf16)

        @pl.loop(0, lat_size)
        def _(part):
            zonal = jnp.dot(table_fwd[0, part], weighted[0], preferred_element_type=f32)
            for block in range(1, lon_size):
                zonal += jnp.dot(table_fwd[block, part], weighted[block], preferred_element_type=f32)
            spectrum = jnp.dot(zonal.astype(bf16), modes_fwd[...], preferred_element_type=f32)
            tapered = (spectrum * taper_all[part].astype(f32)).astype(bf16)
            inverse[part] = jnp.dot(tapered, modes_inv[...], preferred_element_type=f32).astype(bf16)

        @pl.loop(0, lon_size)
        def _(block):
            localized = jnp.dot(table_inv[block, 0], inverse[0], preferred_element_type=f32)
            for part in range(1, lat_size):
                localized += jnp.dot(table_inv[block, part], inverse[part], preferred_element_type=f32)
            for band in range(lat_size):
                total[block, band] += (
                    fields[turn, band, block].astype(f32)
                    * localized[:, band * row_count:(band + 1) * row_count]
                )

    mem_copy = remote(
        total.at[pl.ds((1 - mem) * half, half)], partner_part, mem_sem.at[0], mem_sem.at[1],
        device(lat, lon, 1 - mem),
    )
    mem_copy.start()
    mem_copy.wait_recv()
    for block in range(half):
        for band in range(lat_size):
            lat_send[band, block] = (total[mem * half + block, band] + partner_part[block, band]).astype(bf16)
    lat_copies = [
        remote(
            lat_send.at[lax.rem(lat + step, lat_size)], lat_recv.at[step],
            lat_ss.at[step], lat_rs.at[step], device(lax.rem(lat + step, lat_size), lon, mem),
        )
        for step in range(1, lat_size)
    ]
    for copy in lat_copies:
        copy.start()
    for copy in lat_copies:
        copy.wait_recv()
    for block in range(half):
        summed = lat_send[lat, block].astype(f32)
        for step in range(1, lat_size):
            summed += lat_recv[step, block].astype(f32)
        lon_send[block] = summed.astype(bf16)

    def lon_copy(block):
        return remote(
            lon_send.at[block], lon_recv.at[lon], lon_ss.at[block], lon_rs.at[lon],
            device(lat, mem * half + block, mem),
        )

    def lon_local(block):
        return pltpu.make_async_copy(lon_send.at[block], lon_recv.at[lon], lon_ss.at[block])

    for block in range(half):
        pl.when(mem * half + block != lon)(lambda block=block: lon_copy(block).start())
        pl.when(mem * half + block == lon)(lambda block=block: lon_local(block).start())
    receives = lax.div(lon, half) == mem
    pair_copy = remote(lon_recv, lon_recv, pair_sem.at[0], pair_sem.at[1], device(lat, lon, 1 - mem))

    @pl.when(receives)
    def _():
        for step in range(1, lon_size):
            sender = lax.rem(lon + step, lon_size)
            remote(
                lon_send.at[0], lon_recv.at[sender], lon_ss.at[0], lon_rs.at[sender],
                device(lat, sender, mem),
            ).wait_recv()

    for block in range(half):
        pl.when(mem * half + block != lon)(lambda block=block: lon_copy(block).wait_send())
        pl.when(mem * half + block == lon)(lambda block=block: lon_local(block).wait())

    @pl.when(receives)
    def _():
        pair_copy.start()
        pair_copy.wait_send()

    @pl.when(jnp.logical_not(receives))
    def _():
        pair_copy.wait_recv()

    out[...] = lon_recv[...]
    mem_copy.wait_send()
    for copy in taper_copies + innov_copies + gather_copies + lat_copies:
        copy.wait_send()

    @pl.loop(0, own)
    def _(turn):
        @pl.loop(1, place_count)
        def _(offset):
            field_copy(turn, offset).wait_send()


def local(anomalies, taper, obs_row, obs_col, obs_level, obs_value):
    member_count, level_count, col_count, row_count = anomalies.shape
    lon_size, lat_size = lax.axis_size("lon"), lax.axis_size("lat")
    lon_total, lat_total = col_count * lon_size, row_count * lat_size
    ensemble = member_count * lax.axis_size("mem")
    own = member_count // lat_size
    place_count = lat_size * lon_size
    half = lon_size // 2
    part_count = taper.shape[1]
    lon_table = lon_basis(lon_total).reshape(lon_size, col_count, lat_size, part_count)
    lat_table = lat_basis(lat_total)
    f32, bf16 = jnp.float32, jnp.bfloat16
    slab = (col_count, row_count)
    whole = pl.BlockSpec(memory_space=pl.ANY)
    near = pl.BlockSpec(memory_space=pltpu.VMEM)
    dma = pltpu.SemaphoreType.DMA
    result = pl.pallas_call(
        functools.partial(fused_kernel, lat_size, lon_size, own, obs_row.shape[0]),
        out_shape=jax.ShapeDtypeStruct((level_count,) + slab, bf16),
        in_specs=[whole, whole, near, near, near, near, whole, whole, whole, whole],
        out_specs=near,
        scratch_shapes=[
            pltpu.VMEM((own, lat_size, lon_size) + slab, bf16),
            pltpu.VMEM((lon_size, lat_size, part_count, col_count), bf16),
            pltpu.VMEM((lon_size, lat_size, col_count, part_count), bf16),
            pltpu.VMEM((lat_total, lat_total), bf16),
            pltpu.VMEM((lat_total, lat_total), bf16),
            pltpu.VMEM((lat_size, part_count, lat_total), bf16),
            pltpu.VMEM((level_count, col_count, 2 * row_count), f32),
            pltpu.VMEM((level_count,) + slab, bf16),
            pltpu.VMEM((lat_size, lon_size) + slab, bf16),
            pltpu.VMEM((lon_size, col_count, lat_total), bf16),
            pltpu.VMEM((lat_size, part_count, lat_total), bf16),
            pltpu.VMEM((lon_size, lat_size) + slab, f32),
            pltpu.VMEM((half, lat_size) + slab, f32),
            pltpu.VMEM((lat_size, half) + slab, bf16),
            pltpu.VMEM((lat_size, half) + slab, bf16),
            pltpu.VMEM((half,) + slab, bf16),
            pltpu.VMEM((level_count,) + slab, bf16),
            dma((own, place_count)), dma((own, place_count)), dma((own,)), dma((5,)),
            dma((lat_size,)), dma((lat_size,)), dma((lon_size,)), dma((lon_size,)),
            dma((lat_size,)), dma((lat_size,)), dma((2,)), dma((lat_size,)), dma((lat_size,)),
            dma((half,)), dma((lon_size,)), dma((2,)),
        ],
        compiler_params=pltpu.CompilerParams(
            collective_id=0, has_side_effects=True, vmem_limit_bytes=60 * 1024 * 1024
        ),
    )(
        anomalies, taper[0].astype(bf16), obs_level, obs_col, obs_row, obs_value,
        lon_table.transpose(0, 2, 3, 1), lon_table.transpose(0, 2, 1, 3), lat_table, lat_table.T,
    )
    return result.astype(f32) / (ensemble - 1)


def solution(mesh):
    in_specs = (
        P("mem", None, "lon", "lat"),
        P("lon", "lat", None),
        P("lat", "lon"),
        P("lat", "lon"),
        P("lat", "lon"),
        P("lat", "lon"),
    )
    out_specs = P(None, "lon", "lat")
    return jax.shard_map(local, mesh=mesh, in_specs=in_specs, out_specs=out_specs, check_vma=False)
```

time: 312 us -> 187 us (0.60); the launches traced: 306 us -> 186 us
  Pallas kernels: 0 us -> 145 us
  waiting for transfers between devices: 86.9 us -> 0 us
  matrix products: 86.8 us -> 0 us
  blocking collectives: 77.1 us -> 0 us
  starting transfers between devices: 15 us -> 0 us
  between operations: 13.7 us -> 0.03 us
  local copies, waits for them, and re-layouts: 10.4 us -> 23.3 us
    pallas_call x0 -> x1, Pallas kernels: none -> 145 us  [local(): pl.pallas_call(functools.partial(fused_kernel, lat_size, lon_size, own, o...]
    dot_general x13 -> x0, matrix products: 86.8 us -> none  [the longest x3 36.3 us: local(): jnp.einsum('kn,yn->ky', tapered, lat_table, preferred_element_type=jnp.fl...]
    all_to_all x3 -> x0, blocking collectives: 77.1 us -> none  [the longest x1 40.1 us: local(): lax.all_to_all(grouped[:, turn].reshape(lat_size * lon_size, col_count, r...]
    all_to_all x3 -> x0, waiting for transfers between devices: 69.6 us -> none  [the longest x2 62.7 us: local(): lax.all_to_all(grouped[:, turn].reshape(lat_size * lon_size, col_count, r...]
    convert_element_type x4 -> x3, local copies, waits for them, and re-layouts: 0.07 us -> 23.3 us  [lon_basis(): return basis.reshape(length, length).astype(jnp.bfloat16)]
    psum x1 -> x0, waiting for transfers between devices: 16.6 us -> none  [local(): merged = lax.psum(jnp.sum(parts.astype(jnp.float32), axis=0), 'mem')]
    all_to_all x3 -> x0, starting transfers between devices: 14.5 us -> none  [the longest x2 8.11 us: local(): lax.all_to_all(grouped[:, turn].reshape(lat_size * lon_size, col_count, r...]
    convert_element_type x11 -> x2, other arithmetic: 4.5 us -> 9.65 us  [the longest x1 8.86 us: lat_basis(): return (jnp.cos(angles) * scales).astype(jnp.bfloat16)]
  transfers between devices with their start and end apart: 6 -> 0, of which waited for: 4 -> 0; matrix products, arithmetic and copies ran while one was open for 8% -> 0% of each run, Pallas kernels for 0% -> 0%
where the time goes in v2:
time: 187 us; the launch traced here: 186 us
  Pallas kernels  145 us (78%)
  local copies, waits for them, and re-layouts  23.3 us (12%)
  other arithmetic  17.3 us (9%)
    pallas_call x1, Pallas kernels, local(): pl.pallas_call(functools.partial(fused_kernel, lat_size, lon_size, own, o...  145 us
    convert_element_type x3, local copies, waits for them, and re-layouts, lon_basis(): return basis.reshape(length, length).astype(jnp.bfloat16)  23.3 us
    convert_element_type x1, other arithmetic, lat_basis(): return (jnp.cos(angles) * scales).astype(jnp.bfloat16)  8.86 us

profile of v2, /device:TPU:0, one launch (start us, length us, event | category | flops | bytes accessed | tf_op | source)
XLA Modules:
  0.0 185.9 jit_solution(1156449326794759771)
XLA Ops:
  0.0 1.3 negate_select_fusion.4
  1.4 0.8 fusion.28
  2.2 3.5 %add_convert_fusion = bf16[45,32,1440]{2,1,0:T(8,128)(2,1)} fusion(f32[32,1440]{1,0:T(8,128)S(1)} %get-tuple-element.12, f32[45,1440]{1,0:T(8,128)S(1)} %get-tuple-element.11, f32[32,1440]{1,0:T(8,128)S(1)} %get-tuple-element.10, f32[45,1440]{1,0:T(8,128)S(1)} %get-tuple-element.9), kind=kLoop, calls=%fused_computation | loop fusion | flops 8294400 | bytes 5034240 | tf_op jit(solution)/shard_map/convert_element_type | solution.py:34
  5.7 10.2 %convert_element_type.41 = bf16[4,360,4,360]{3,2,1,0:T(4,128)(2,1)} reshape(bf16[45,32,1440]{2,1,0:T(8,128)(2,1)} %add_convert_fusion) | data formatting | bytes 8294400 | tf_op jit(solution)/shard_map/convert_element_type | solution.py:34
  16.0 8.1 %copy.8 = bf16[4,360,4,360]{1,3,2,0:T(8,128)(2,1)} copy(bf16[4,360,4,360]{3,2,1,0:T(4,128)(2,1)} %convert_element_type.41) | data formatting | bytes 8294400 | tf_op jit(solution)/shard_map/convert_element_type | solution.py:34
  24.0 0.0 copy-start
  24.0 5.0 %copy.11 = bf16[4,360,4,360]{3,1,2,0:T(8,128)(2,1)} copy(bf16[4,360,4,360]{3,2,1,0:T(4,128)(2,1)} %convert_element_type.41) | data formatting | bytes 8294400 | tf_op jit(solution)/shard_map/convert_element_type | solution.py:34
  29.0 8.9 %fusion.11 = (bf16[512,512]{1,0:T(8,128)(2,1)}, bf16[512,512]{1,0:T(8,128)(2,1)}) fusion(f32[512]{0:T(512)S(1)} %fusion.33, s32[512]{0:T(512)S(1)} %multiply_add_fusion), kind=kLoop, calls=%fused_computation.19 | loop fusion | flops 8388608 | bytes 1052672 | tf_op jit(solution)/shard_map/convert_element_type | solution.py:43
  37.9 0.0 copy-done
  37.9 0.8 convert_bitcast_fusion.taper
  38.7 145.3 %shard_map.64 = bf16[4,360,128]{2,1,0:T(8,128)(2,1)} custom-call(bf16[12,4,360,128]{3,2,1,0:T(8,128)(2,1)} %anom.1, bf16[360,512]{1,0:T(8,128)(2,1)} %convert_bitcast_fusion.taper, s32[64,128]{1,0:T(8,128)} %level.1, s32[64,128]{1,0:T(8,128)} %column.1, s32[64,128]{1,0:T(8,128)} %row.1, f32[64,128]{1,0:T(8,128)} %value.1, bf16[4,4,360,360]{3,2,1,0:T(8,128)(2,1)} %bitcast.6, ...), custom_call_target="tpu_custom_call" | custom-call | tf_op jit(solution)/shard_map/pallas_call | solution.py:314
  184.0 1.9 %convert_multiply_fusion = f32[4,360,128]{2,1,0:T(8,128)} fusion(bf16[4,360,128]{2,1,0:T(8,128)(2,1)} %shard_map.64), kind=kLoop, calls=%fused_computation.26 | loop fusion | flops 368640 | bytes 1105920 | tf_op jit(solution)/shard_map/div | solution.py:349
  (6 shorter events, 0.0 us)
Async XLA Ops:
  24.0 13.8 %copy-start = (f32[1,360,512]{2,1,0:T(8,128)S(1)}, f32[1,360,512]{2,1,0:T(8,128)}, u32[]{:S(2)}) copy-start(f32[1,360,512]{2,1,0:T(8,128)} %param.7) | copy-start | bytes 2211844

commit v3 on v2

--- a/solution.py
+++ b/solution.py
@@ -8,30 +8,35 @@
 from jax.experimental.pallas import tpu as pltpu
 from jax.sharding import PartitionSpec as P
 
-def lon_basis(length):
+
+def lon_factors(block_count, block_size, part_count, part_size):
+    length = block_count * block_size
     nyquist = length // 2
-    inner = next(size for size in range(32, 0, -1) if length % size == 0)
-    outer = length // inner
-    coef_idx = jnp.arange(length, dtype=jnp.int32)
+    inner = 24 if block_size % 24 == 0 else next(n for n in range(32, 0, -1) if block_size % n == 0)
+    outer = block_size // inner
+    coef_idx = jnp.arange(length, dtype=jnp.int32).reshape(part_count, part_size)
     wavenum = jnp.where(coef_idx <= nyquist, coef_idx, coef_idx - nyquist)
-    step = 2.0 * math.pi / length
-
-    def angles(points):
-        return (points[:, None] * wavenum[None, :] % length).astype(jnp.float32) * step
-
-    coarse = angles(jnp.arange(outer, dtype=jnp.int32) * inner)
-    fine = angles(jnp.arange(inner, dtype=jnp.int32))
+
+    def waves(points, coefs):
+        phase_idx = points * coefs % length
+        angles = phase_idx.astype(jnp.float32) * (2.0 * math.pi / length)
+        return jnp.cos(angles), jnp.sin(angles)
+
     scales = jnp.where(
         (coef_idx == 0) | (coef_idx == nyquist), 1.0 / math.sqrt(length), math.sqrt(2.0 / length)
     )
-    is_cos = (coef_idx <= nyquist)[None, :]
-    coarse_cos, coarse_sin = jnp.cos(coarse) * scales, jnp.sin(coarse) * scales
-    fine_cos, fine_sin = jnp.cos(fine), jnp.sin(fine)
-    first = jnp.where(is_cos, coarse_cos, coarse_sin)
-    second = jnp.where(is_cos, -coarse_sin, coarse_cos)
-    first, second, fine_cos, fine_sin = lax.optimization_barrier((first, second, fine_cos, fine_sin))
-    basis = first[:, None, :] * fine_cos[None] + second[:, None, :] * fine_sin[None]
-    return basis.reshape(length, length).astype(jnp.bfloat16)
+    starts = (jnp.arange(block_count, dtype=jnp.int32) * block_size)[:, None, None]
+    start_cos, start_sin = waves(starts, wavenum[None])
+    is_cos = (coef_idx <= nyquist)[None]
+    first = jnp.where(is_cos, start_cos, start_sin) * scales
+    second = jnp.where(is_cos, -start_sin, start_cos) * scales
+    coarse = jnp.stack([first, second], axis=2)
+    high = (jnp.arange(outer, dtype=jnp.int32) * inner)[None, :, None, None]
+    low = jnp.arange(inner, dtype=jnp.int32)[None, None, :, None]
+    pieces = waves(high, wavenum[:, None, None, :]) + waves(low, wavenum[:, None, None, :])
+    high_cos, high_sin, low_cos, low_sin = lax.optimization_barrier(pieces)
+    fine = jnp.stack([high_cos * low_cos - high_sin * low_sin, high_sin * low_cos + high_cos * low_sin])
+    return coarse, fine.reshape(2, part_count, block_size, part_size)
 
 
 def lat_basis(length):
@@ -45,8 +50,8 @@
 
 def fused_kernel(
     lat_size, lon_size, own, obs_rows,
-    anom, taper, level, column, row, value, lon_fwd, lon_inv, lat_fwd, lat_inv, out,
-    fields, table_fwd, table_inv, modes_fwd, modes_inv, taper_all, hits, innov_own, innov_all,
+    anom, taper, level, column, row, value, coarse, fine, modes, out,
+    fields, table_fwd, table_inv, fine_near, modes_near, taper_near, taper_all, hits, innov_own, innov_all,
     weighted, inverse, total, partner_part, lat_send, lat_recv, lon_send, lon_recv,
     field_ss, field_rs, local_sem, table_sem, taper_ss, taper_rs, innov_ss, innov_rs,
     gather_ss, gather_rs, mem_sem, lat_ss, lat_rs, lon_ss, lon_rs, pair_sem,
@@ -107,7 +112,7 @@
     send_fields(0)
     taper_copies = [
         remote(
-            taper, taper_all.at[lat], taper_ss.at[step], taper_rs.at[step],
+            taper_all.at[lat], taper_all.at[lat], taper_ss.at[step], taper_rs.at[step],
             device(lax.rem(lat + step, lat_size), lon, mem),
         )
         for step in range(1, lat_size)
@@ -115,8 +120,7 @@
     table_copies = [
         pltpu.make_async_copy(src, dst, table_sem.at[idx])
         for idx, (src, dst) in enumerate([
-            (lon_fwd, table_fwd), (lon_inv, table_inv), (lat_fwd, modes_fwd),
-            (lat_inv, modes_inv), (taper, taper_all.at[lat]),
+            (taper.at[0], taper_near), (fine, fine_near), (modes, modes_near),
         ])
     ]
     for copy in table_copies:
@@ -163,9 +167,24 @@
         copy.start()
     innov_local = pltpu.make_async_copy(innov_own.at[lon], innov_all.at[lat, lon], innov_ss.at[0])
     innov_local.start()
+    table_copies[0].wait()
+    taper_all[lat] = taper_near[...].astype(bf16)
     for copy in taper_copies:
         copy.start()
     send_fields(1)
+    for copy in table_copies[1:]:
+        copy.wait()
+
+    @pl.loop(0, lon_size)
+    def _(block):
+        for part in range(lat_size):
+            table = (
+                coarse[block, part, 0:1, :] * fine_near[0, part]
+                + coarse[block, part, 1:2, :] * fine_near[1, part]
+            )
+            table_inv[block, part] = table.astype(bf16)
+            table_fwd[block, part] = table.T.astype(bf16)
+
     innov_local.wait()
     for copy in innov_copies:
         copy.wait_recv()
@@ -181,36 +200,42 @@
     for turn in range(2, own):
         send_fields(turn)
     total[...] = jnp.zeros_like(total)
-    for copy in table_copies:
-        copy.wait()
     for copy in taper_copies + gather_copies:
         copy.wait_recv()
 
+    mem_copy = remote(
+        total.at[pl.ds((1 - mem) * half, half)], partner_part, mem_sem.at[0], mem_sem.at[1],
+        device(lat, lon, 1 - mem),
+    )
+
     @pl.loop(0, own)
     def _(turn):
+        def weigh(band, block):
+            product = fields[turn, band, block].astype(f32) * innov_all[band, block].astype(f32)
+            lanes = pl.ds(pl.multiple_of(band * row_count, row_count), row_count)
+            weighted[block, :, lanes] = product.astype(bf16)
+
         own_copy(turn).wait()
+        weigh(lat, lon)
 
         @pl.loop(1, place_count)
         def _(offset):
             field_copy(turn, offset).wait_recv()
-
-        @pl.loop(0, lon_size)
-        def _(block):
-            for band in range(lat_size):
-                product = fields[turn, band, block].astype(f32) * innov_all[band, block].astype(f32)
-                weighted[block, :, band * row_count:(band + 1) * row_count] = product.astype(bf16)
+            weigh(*place(place_count - offset))
 
         @pl.loop(0, lat_size)
         def _(part):
             zonal = jnp.dot(table_fwd[0, part], weighted[0], preferred_element_type=f32)
             for block in range(1, lon_size):
                 zonal += jnp.dot(table_fwd[block, part], weighted[block], preferred_element_type=f32)
-            spectrum = jnp.dot(zonal.astype(bf16), modes_fwd[...], preferred_element_type=f32)
+            spectrum = jnp.dot(zonal.astype(bf16), modes_near[...], preferred_element_type=f32)
             tapered = (spectrum * taper_all[part].astype(f32)).astype(bf16)
-            inverse[part] = jnp.dot(tapered, modes_inv[...], preferred_element_type=f32).astype(bf16)
-
-        @pl.loop(0, lon_size)
-        def _(block):
+            inverse[part] = lax.dot_general(
+                tapered, modes_near[...], (((1,), (1,)), ((), ())), preferred_element_type=f32
+            ).astype(bf16)
+
+        def localize(step):
+            block = lax.rem((1 - mem) * half + step, lon_size)
             localized = jnp.dot(table_inv[block, 0], inverse[0], preferred_element_type=f32)
             for part in range(1, lat_size):
                 localized += jnp.dot(table_inv[block, part], inverse[part], preferred_element_type=f32)
@@ -220,31 +245,27 @@
                     * localized[:, band * row_count:(band + 1) * row_count]
                 )
 
-    mem_copy = remote(
-        total.at[pl.ds((1 - mem) * half, half)], partner_part, mem_sem.at[0], mem_sem.at[1],
-        device(lat, lon, 1 - mem),
-    )
-    mem_copy.start()
+        pl.loop(0, half)(localize)
+        pl.when(turn == own - 1)(lambda: mem_copy.start())
+        pl.loop(half, lon_size)(localize)
+
     mem_copy.wait_recv()
+    lat_copies = [
+        [
+            remote(
+                lat_send.at[block, lax.rem(lat + step, lat_size)], lat_recv.at[block, step],
+                lat_ss.at[block, step], lat_rs.at[block, step],
+                device(lax.rem(lat + step, lat_size), lon, mem),
+            )
+            for step in range(1, lat_size)
+        ]
+        for block in range(half)
+    ]
     for block in range(half):
         for band in range(lat_size):
-            lat_send[band, block] = (total[mem * half + block, band] + partner_part[block, band]).astype(bf16)
-    lat_copies = [
-        remote(
-            lat_send.at[lax.rem(lat + step, lat_size)], lat_recv.at[step],
-            lat_ss.at[step], lat_rs.at[step], device(lax.rem(lat + step, lat_size), lon, mem),
-        )
-        for step in range(1, lat_size)
-    ]
-    for copy in lat_copies:
-        copy.start()
-    for copy in lat_copies:
-        copy.wait_recv()
-    for block in range(half):
-        summed = lat_send[lat, block].astype(f32)
-        for step in range(1, lat_size):
-            summed += lat_recv[step, block].astype(f32)
-        lon_send[block] = summed.astype(bf16)
+            lat_send[block, band] = (total[mem * half + block, band] + partner_part[block, band]).astype(bf16)
+        for copy in lat_copies[block]:
+            copy.start()
 
     def lon_copy(block):
         return remote(
@@ -256,6 +277,12 @@
         return pltpu.make_async_copy(lon_send.at[block], lon_recv.at[lon], lon_ss.at[block])
 
     for block in range(half):
+        for copy in lat_copies[block]:
+            copy.wait_recv()
+        summed = lat_send[block, lat].astype(f32)
+        for step in range(1, lat_size):
+            summed += lat_recv[block, step].astype(f32)
+        lon_send[block] = summed.astype(bf16)
         pl.when(mem * half + block != lon)(lambda block=block: lon_copy(block).start())
         pl.when(mem * half + block == lon)(lambda block=block: lon_local(block).start())
     receives = lax.div(lon, half) == mem
@@ -285,7 +312,7 @@
 
     out[...] = lon_recv[...]
     mem_copy.wait_send()
-    for copy in taper_copies + innov_copies + gather_copies + lat_copies:
+    for copy in taper_copies + innov_copies + gather_copies + sum(lat_copies, []):
         copy.wait_send()
 
     @pl.loop(0, own)
@@ -304,7 +331,7 @@
     place_count = lat_size * lon_size
     half = lon_size // 2
     part_count = taper.shape[1]
-    lon_table = lon_basis(lon_total).reshape(lon_size, col_count, lat_size, part_count)
+    coarse, fine = lon_factors(lon_size, col_count, lat_size, part_count)
     lat_table = lat_basis(lat_total)
     f32, bf16 = jnp.float32, jnp.bfloat16
     slab = (col_count, row_count)
@@ -314,14 +341,15 @@
     result = pl.pallas_call(
         functools.partial(fused_kernel, lat_size, lon_size, own, obs_row.shape[0]),
         out_shape=jax.ShapeDtypeStruct((level_count,) + slab, bf16),
-        in_specs=[whole, whole, near, near, near, near, whole, whole, whole, whole],
+        in_specs=[whole, whole, near, near, near, near, near, whole, whole],
         out_specs=near,
         scratch_shapes=[
             pltpu.VMEM((own, lat_size, lon_size) + slab, bf16),
             pltpu.VMEM((lon_size, lat_size, part_count, col_count), bf16),
             pltpu.VMEM((lon_size, lat_size, col_count, part_count), bf16),
+            pltpu.VMEM((2, lat_size, col_count, part_count), f32),
             pltpu.VMEM((lat_total, lat_total), bf16),
-            pltpu.VMEM((lat_total, lat_total), bf16),
+            pltpu.VMEM((part_count, lat_total), f32),
             pltpu.VMEM((lat_size, part_count, lat_total), bf16),
             pltpu.VMEM((level_count, col_count, 2 * row_count), f32),
             pltpu.VMEM((level_count,) + slab, bf16),
@@ -330,21 +358,20 @@
             pltpu.VMEM((lat_size, part_count, lat_total), bf16),
             pltpu.VMEM((lon_size, lat_size) + slab, f32),
             pltpu.VMEM((half, lat_size) + slab, f32),
-            pltpu.VMEM((lat_size, half) + slab, bf16),
-            pltpu.VMEM((lat_size, half) + slab, bf16),
+            pltpu.VMEM((half, lat_size) + slab, bf16),
+            pltpu.VMEM((half, lat_size) + slab, bf16),
             pltpu.VMEM((half,) + slab, bf16),
             pltpu.VMEM((level_count,) + slab, bf16),
-            dma((own, place_count)), dma((own, place_count)), dma((own,)), dma((5,)),
+            dma((own, place_count)), dma((own, place_count)), dma((own,)), dma((3,)),
             dma((lat_size,)), dma((lat_size,)), dma((lon_size,)), dma((lon_size,)),
-            dma((lat_size,)), dma((lat_size,)), dma((2,)), dma((lat_size,)), dma((lat_size,)),
+            dma((lat_size,)), dma((lat_size,)), dma((2,)), dma((half, lat_size)), dma((half, lat_size)),
             dma((half,)), dma((lon_size,)), dma((2,)),
         ],
         compiler_params=pltpu.CompilerParams(
             collective_id=0, has_side_effects=True, vmem_limit_bytes=60 * 1024 * 1024
         ),
     )(
-        anomalies, taper[0].astype(bf16), obs_level, obs_col, obs_row, obs_value,
-        lon_table.transpose(0, 2, 3, 1), lon_table.transpose(0, 2, 1, 3), lat_table, lat_table.T,
+        anomalies, taper, obs_level, obs_col, obs_row, obs_value, coarse, fine, lat_table,
     )
     return result.astype(f32) / (ensemble - 1)
 

time: 187 us -> 155 us (0.83)
  local copies, waits for them, and re-layouts: 23.3 us -> 0 us
  other arithmetic: 17.3 us -> 12.4 us
  Pallas kernels: 145 us -> 142 us
    convert_element_type x3 -> x0, local copies, waits for them, and re-layouts: 23.3 us -> none  [lon_basis(): return basis.reshape(length, length).astype(jnp.bfloat16)]
    convert_element_type x2 -> x0, other arithmetic: 4.31 us -> none  [the longest x1 3.52 us: lon_basis(): return basis.reshape(length, length).astype(jnp.bfloat16)]
    convert_element_type x1, other arithmetic: 8.86 us -> 4.89 us  [lat_basis(): return (jnp.cos(angles) * scales).astype(jnp.bfloat16)]
    pallas_call x1, Pallas kernels: 145 us -> 142 us  [local(): pl.pallas_call(functools.partial(fused_kernel, lat_size, lon_size, own, o...]
    another operation x0 -> x2, other arithmetic: none -> 2.98 us  [the longest x1 2.32 us: lon_factors(): jnp.stack([high_cos * low_cos - high_sin * low_sin, high_sin * low_cos +...]
where the time goes in v3:
time: 155 us; the launch traced here: 154 us
  Pallas kernels  142 us (92%)
  other arithmetic  12.4 us (8%)
    pallas_call x1, Pallas kernels, local(): pl.pallas_call(functools.partial(fused_kernel, lat_size, lon_size, own, o...  142 us
    convert_element_type x1, other arithmetic, lat_basis(): return (jnp.cos(angles) * scales).astype(jnp.bfloat16)  4.89 us

profile of v3, /device:TPU:0, one launch (start us, length us, event | category | flops | bytes accessed | tf_op | source)
XLA Modules:
  0.0 154.4 jit_solution(15729616949411056010)
XLA Ops:
  0.0 0.6 fusion.13
  0.6 0.5 fusion.20
  1.1 0.5 multiply_subtract_fusion
  1.7 2.3 %pad_maximum_fusion.fine = f32[2,4,360,360]{3,2,1,0:T(8,128)} fusion(f32[1,4,360,360]{3,2,1,0:T(8,128)S(1)} %bitcast.7, f32[1,4,360,360]{3,2,1,0:T(8,128)S(1)} %bitcast.6), kind=kLoop, calls=%fused_computation | loop fusion | flops 1036800 | bytes 8294400 | tf_op jit(solution)/shard_map/stack | solution.py:38
  4.0 0.9 fusion.23
  4.9 0.7 pad_maximum_fusion.1.coarse
  5.6 4.9 %fusion.5.modes = bf16[512,512]{1,0:T(8,128)(2,1)} fusion(f32[512]{0:T(512)S(1)} %fusion.32, s32[512]{0:T(512)S(1)} %multiply_add_fusion.2), kind=kLoop, calls=%fused_computation.11 | loop fusion | flops 4194304 | bytes 528384 | tf_op jit(solution)/shard_map/convert_element_type | solution.py:48
  10.5 142.0 %shard_map.64 = bf16[4,360,128]{2,1,0:T(8,128)(2,1)} custom-call(bf16[12,4,360,128]{3,2,1,0:T(8,128)(2,1)} %anom.1, f32[1,360,512]{2,1,0:T(8,128)} %taper.1, s32[64,128]{1,0:T(8,128)} %level.1, s32[64,128]{1,0:T(8,128)} %column.1, s32[64,128]{1,0:T(8,128)} %row.1, f32[64,128]{1,0:T(8,128)} %value.1, f32[4,4,2,360]{3,2,1,0:T(2,128)} %pad_maximum_fusion.1.coarse, ...), custom_call_target="tpu_custom_call" | custom-call | tf_op jit(solution)/shard_map/pallas_call | solution.py:341
  152.5 1.9 %convert_multiply_fusion = f32[4,360,128]{2,1,0:T(8,128)} fusion(bf16[4,360,128]{2,1,0:T(8,128)(2,1)} %shard_map.64), kind=kLoop, calls=%fused_computation.15 | loop fusion | flops 368640 | bytes 1105920 | tf_op jit(solution)/shard_map/div | solution.py:376
  (7 shorter events, 0.0 us)

commit v4 on v3

--- a/solution.py
+++ b/solution.py
@@ -40,12 +40,23 @@
 
 
 def lat_basis(length):
-    grid_idx = jnp.arange(length, dtype=jnp.int32)[:, None]
+    inner = next(size for size in range(32, 0, -1) if length % size == 0)
+    outer = length // inner
     mode_idx = jnp.arange(length, dtype=jnp.int32)[None, :]
-    phase_idx = mode_idx * (2 * grid_idx + 1) % (4 * length)
-    angles = phase_idx.astype(jnp.float32) * (math.pi / (2.0 * length))
+
+    def waves(points):
+        phase_idx = mode_idx * points[:, None] % (4 * length)
+        angles = phase_idx.astype(jnp.float32) * (math.pi / (2.0 * length))
+        return jnp.cos(angles), jnp.sin(angles)
+
     scales = jnp.where(mode_idx == 0, 1.0 / math.sqrt(length), math.sqrt(2.0 / length))
-    return (jnp.cos(angles) * scales).astype(jnp.bfloat16)
+    high_cos, high_sin = waves(jnp.arange(outer, dtype=jnp.int32) * (2 * inner))
+    low_cos, low_sin = waves(jnp.arange(inner, dtype=jnp.int32) * 2 + 1)
+    high_cos, high_sin, low_cos, low_sin = lax.optimization_barrier(
+        (high_cos * scales, high_sin * scales, low_cos, low_sin)
+    )
+    basis = high_cos[:, None, :] * low_cos[None] - high_sin[:, None, :] * low_sin[None]
+    return basis.reshape(length, length).astype(jnp.bfloat16)
 
 
 def fused_kernel(

time: 155 us -> 152 us (0.981)
  other arithmetic: 12.4 us -> 8.99 us
    convert_element_type x1, other arithmetic: 4.89 us -> 0.96 us  [lat_basis(): return basis.reshape(length, length).astype(jnp.bfloat16)]
where the time goes in v4:
time: 152 us; the launch traced here: 151 us
  Pallas kernels  142 us (93%)
  other arithmetic  8.99 us (6%)
    pallas_call x1, Pallas kernels, local(): pl.pallas_call(functools.partial(fused_kernel, lat_size, lon_size, own, o...  142 us

profile of v4, /device:TPU:0, one launch (start us, length us, event | category | flops | bytes accessed | tf_op | source)
XLA Modules:
  0.0 151.1 jit_solution(9094909221047684432)
XLA Ops:
  0.0 0.6 fusion.4
  0.6 0.5 fusion.11
  1.1 0.5 multiply_subtract_fusion
  1.7 2.3 %pad_maximum_fusion.fine = f32[2,4,360,360]{3,2,1,0:T(8,128)} fusion(f32[1,4,360,360]{3,2,1,0:T(8,128)S(1)} %bitcast.8, f32[1,4,360,360]{3,2,1,0:T(8,128)S(1)} %bitcast.7), kind=kLoop, calls=%fused_computation | loop fusion | flops 1036800 | bytes 8294400 | tf_op jit(solution)/shard_map/stack | solution.py:38
  4.0 0.3 fusion.23
  4.3 0.2 sine_multiply_fusion
  4.6 1.0 subtract_convert_fusion
  5.5 0.9 fusion.28
  6.5 0.7 pad_maximum_fusion.1.coarse
  7.1 142.0 %shard_map.64 = bf16[4,360,128]{2,1,0:T(8,128)(2,1)} custom-call(bf16[12,4,360,128]{3,2,1,0:T(8,128)(2,1)} %anom.1, f32[1,360,512]{2,1,0:T(8,128)} %taper.1, s32[64,128]{1,0:T(8,128)} %level.1, s32[64,128]{1,0:T(8,128)} %column.1, s32[64,128]{1,0:T(8,128)} %row.1, f32[64,128]{1,0:T(8,128)} %value.1, f32[4,4,2,360]{3,2,1,0:T(2,128)} %pad_maximum_fusion.1.coarse, ...), custom_call_target="tpu_custom_call" | custom-call | tf_op jit(solution)/shard_map/pallas_call | solution.py:352
  149.2 1.9 %convert_multiply_fusion = f32[4,360,128]{2,1,0:T(8,128)} fusion(bf16[4,360,128]{2,1,0:T(8,128)(2,1)} %shard_map.64), kind=kLoop, calls=%fused_computation.4 | loop fusion | flops 368640 | bytes 1105920 | tf_op jit(solution)/shard_map/div | solution.py:387
  (8 shorter events, 0.0 us)
